TPU v7x, 32 devices: a whole 2x2x4 slice. The times are simulated.
32 devices in a mesh: pole: 2 (over y), prow: 4 (over z), pcol: 4 (over x, core).
Axes of the slice: x: 2, y: 2, z: 4, core: 2. Of those that a mesh axis runs over, the one named last changes fastest.
Arguments:
- ainv_anc: bfloat16 [2, 4096, 2048], P(None, ('pole', 'prow'), 'pcol'), parts along dimension 1, may hold values from -6 to 6
- panel: bfloat16 [2, 8, 1024, 256], P(None, 'pole', ('pcol', 'prow')), parts along dimension 1, may hold values from -6 to 6
- u_inv: bfloat16 [2, 8, 256, 256], P(None, 'pole'), parts along dimension 1, may hold values from -0.01171875 to 0.01171875
- k_inv: float32 [2, 8, 256, 256], P(None, ('pole', 'pcol')), parts along dimension 1, may hold values from -6 to 6
- structure: int32 [4, 4], replicated, may hold values from -1 to 7, as said below
Outputs:
- sel_inv: float32 [2, 4096, 1024], P(None, ('pole', 'prow'), 'pcol'), parts along dimension 1
- diag_inv: float32 [2, 8, 256, 256], P(None, ('pole', 'pcol')), parts along dimension 1
There are 2 independent parts, one for each index of `pole`. A program takes and returns all parts, laid end to end along the dimension named above; an argument that names none is the same for every part. Nothing has to cross between parts.
Inputs may be any that keep to these rules, and one draw needn't show every extreme that they name: `structure`: slots g * 1 to (g + 1) * 1 - 1 of row k hold distinct blocks of g * 2 to (g + 1) * 2 - 1 in rising order, followed by -1 for empty slots; each such group of each row holds at least one block, and for every g some row fills all 1 slots of group g.
All inputs are finite; a program needn't handle non-finite values.
Results may differ from a plain program's by a relative error of at most 0.005.
Values may be sent and summed in bfloat16 or wider, within the bound.
No kernel may reach another device: no remote copies, remote signals or barrier semaphores. Data moves between devices by JAX's collectives and lax.ppermute only.
A program may use at most 128 MiB of HBM per device.

v0:
```python
import jax
import jax.numpy as jnp
from jax import lax
from jax.sharding import PartitionSpec as P


def complex_quad(z_part, s_part):
    highest = lax.Precision.HIGHEST

    def single(left, right):
        return jnp.einsum("kra,rkb->kab", left, right, precision=highest)

    real = single(z_part[0], s_part[0]) - single(z_part[1], s_part[1])
    imag = single(z_part[0], s_part[1]) + single(z_part[1], s_part[0])
    return jnp.stack([real, imag])


def local(ainv_anc, panel, u_inv, k_inv, structure):
    block_width = u_inv.shape[-1]
    total_k = u_inv.shape[1]
    own_k = k_inv.shape[1]
    n_cols = lax.axis_size("pcol")
    row_here = lax.axis_index("prow")
    col_here = lax.axis_index("pcol")
    row_blocks = ainv_anc.shape[1] // block_width
    group_blocks = ainv_anc.shape[2] // block_width
    group_slots = structure.shape[1] // n_cols
    rows_all = row_blocks * block_width
    col_struct = lax.dynamic_slice_in_dim(structure, col_here * group_slots, group_slots, 1)
    slot_live = col_struct >= 0
    slot_pos = col_struct - col_here * group_blocks
    first_block = row_here * row_blocks
    target = first_block + jnp.arange(row_blocks, dtype=jnp.int32)
    rows_in = lax.all_gather(panel, "prow", axis=2, tiled=True)

    def single(left, right):
        return jnp.einsum("knb,kbc->knc", left, right, preferred_element_type=jnp.float32)

    real = single(rows_in[0], u_inv[0]) - single(rows_in[1], u_inv[1])
    imag = single(rows_in[0], u_inv[1]) + single(rows_in[1], u_inv[0])
    placed = jnp.stack([real, imag]).astype(jnp.bfloat16)
    placed = placed.reshape(2, total_k, group_slots, block_width, block_width)
    placed = jnp.where(slot_live[None, :, :, None, None], placed, jnp.zeros((), jnp.bfloat16))
    block_ids = jnp.arange(group_blocks, dtype=jnp.int32)
    pick_table = (slot_pos[:, :, None] == block_ids[None, None, :]).astype(jnp.bfloat16)
    ainv_blocks = ainv_anc.reshape(2, rows_all, group_blocks, block_width)

    def one_node(items):
        table_k, rows_k = items
        picked = jnp.einsum(
            "sg,cigw->cisw", table_k, ainv_blocks, preferred_element_type=jnp.float32
        )
        picked = picked.astype(jnp.bfloat16).reshape(2, rows_all, group_slots * block_width)
        right = rows_k.reshape(2, group_slots * block_width, block_width)
        real = jnp.dot(picked[0], right[0], preferred_element_type=jnp.float32) - jnp.dot(
            picked[1], right[1], preferred_element_type=jnp.float32
        )
        imag = jnp.dot(picked[0], right[1], preferred_element_type=jnp.float32) + jnp.dot(
            picked[1], right[0], preferred_element_type=jnp.float32
        )
        return jnp.stack([real, imag])

    per_node = lax.map(one_node, (pick_table, jnp.moveaxis(placed, 1, 0)))
    partial_value = jnp.transpose(per_node, (1, 2, 0, 3))
    row_table = (col_struct[:, None, :] == target[None, :, None]).astype(jnp.bfloat16)
    z_rows = jnp.einsum("kts,ckswb->cktwb", row_table, placed, preferred_element_type=jnp.float32)
    z_rows = z_rows.astype(jnp.bfloat16).reshape(2, total_k, rows_all, block_width)
    summed = lax.psum_scatter(
        partial_value.reshape(2, rows_all, total_k * block_width),
        "pcol",
        scatter_dimension=2,
        tiled=True,
    )
    own_struct = lax.dynamic_slice_in_dim(structure, col_here * own_k, own_k, 0)
    member = jnp.any(own_struct[:, :, None] == target[None, None, :], axis=1)
    selected = -summed.reshape(2, row_blocks, block_width, own_k, block_width)
    selected = jnp.where(member.T[None, :, None, :, None], selected, 0.0)
    sel_inv = selected.reshape(2, rows_all, own_k * block_width)
    received = lax.all_to_all(z_rows, "pcol", split_axis=1, concat_axis=1, tiled=True)
    z_own = (
        received.astype(jnp.float32).reshape(2, n_cols, own_k, rows_all, block_width).sum(axis=1)
    )
    quad_term = complex_quad(z_own, selected.reshape(2, rows_all, own_k, block_width))
    total_sum = lax.psum(quad_term, "prow")
    diag_inv = k_inv - total_sum
    return (sel_inv, diag_inv)


def solution(mesh):
    placed = (
        P(None, ("pole", "prow"), "pcol"),
        P(None, "pole", ("pcol", "prow"), None),
        P(None, "pole", None, None),
        P(None, ("pole", "pcol"), None, None),
        P(),
    )
    return jax.shard_map(
        local,
        mesh=mesh,
        in_specs=placed,
        out_specs=(P(None, ("pole", "prow"), "pcol"), P(None, ("pole", "pcol"), None, None)),
        check_vma=False,
    )
```

profile of v0, /device:TPU:0, one launch (start us, length us, event | category | flops | bytes accessed | tf_op | source)
XLA Modules:
  0.0 170.8 jit_solution(10218093751577018464)
XLA Ops:
  8.0 1.3 reshape.276
  11.2 29.1 %all-gather.2.cloned.1.call-done = bf16[2,4,256,256]{3,2,1,0:T(8,128)(2,1)} async-done(((bf16[2,4,64,256]{3,2,1,0:T(8,128)(2,1)}), bf16[2,4,256,256]{3,2,1,0:T(8,128)(2,1)}) %all-gather.2.cloned.1.call-update) | async-done | bytes 1048592 | tf_op jit(solution)/shard_map/all_gather | solution.py:34
  40.3 1.6 fusion.13
  41.9 1.3 fusion.17
  44.1 13.4 %while.10 = (s32[]{:T(128)}, f32[4,2,512,256]{3,2,1,0:T(8,128)}, bf16[4,1,2]{2,1,0:T(2,128)(2,1)S(1)}, bf16[2,512,2,256]{3,2,1,0:T(2,128)(2,1)S(1)}, bf16[4,2,1,256,256]{4,3,0,2,1:T(8,128)(2,1)S(1)}, /*index=5*/s32[]{:T(128)}) while((s32[]{:T(128)}, f32[4,2,512,256]{3,2,1,0:T(8,128)}, bf16[4,1,2]{2,1,0:T(2,128)(2,1)S(1)}, ...), condition=%wide.region_2.3_spmd, body=%wide.region_1.2_spmd.sunk | while | flops 270008320 | bytes 9962073 | solution.py:63
  44.1 1.2 fusion.42
  46.4 1.0 fusion.47
  47.4 1.2 fusion.42
  49.7 1.1 fusion.47
  50.8 1.2 fusion.42
  53.1 1.1 fusion.47
  54.2 1.2 fusion.42
  56.4 1.0 fusion.47
  57.5 4.8 %copy.21 = f32[4,2,64,8,256]{4,3,0,2,1:T(8,128)} copy(f32[4,2,64,8,256]{4,3,2,1,0:T(8,128)} %bitcast.135) | data formatting | bytes 8388608 | tf_op jit(solution)/shard_map/reshape | solution.py:69
  63.0 1.5 copy.17
  64.5 3.8 %all-to-all-start = ((bf16[2,4,512,256]{3,2,0,1:T(8,128)(2,1)}), bf16[2,4,512,256]{3,2,0,1:T(8,128)(2,1)S(1)}, u32[]{:S(2)}, u32[]{:S(2)}) async-start(bf16[2,4,512,256]{3,2,0,1:T(8,128)(2,1)} %copy.17), calls=%async_computation.1 | async-start | bytes 4194304 | tf_op jit(solution)/shard_map/all_to_all | solution.py:79
  69.2 36.9 %all-to-all-done = bf16[2,4,512,256]{3,2,0,1:T(8,128)(2,1)S(1)} async-done(((bf16[2,4,512,256]{3,2,0,1:T(8,128)(2,1)}), bf16[2,4,512,256]{3,2,0,1:T(8,128)(2,1)S(1)}, u32[]{:S(2)}, u32[]{:S(2)}) %all-to-all-start) | async-done | bytes 2097184 | tf_op jit(solution)/shard_map/all_to_all | solution.py:79
  106.4 11.5 %reduce-scatter.2.cloned.1.call-done = f32[2,512,256]{2,1,0:T(8,128)} async-done(((f32[2,512,1024]{2,1,0:T(8,128)}), f32[2,512,256]{2,1,0:T(8,128)}) %reduce-scatter.2.cloned.1.call-update) | async-done | bytes 1048592 | tf_op jit(solution)/shard_map/reduce_scatter | solution.py:68
  117.9 2.3 %fusion.26 = (f32[2,512,256]{2,1,0:T(8,128)S(1)}, f32[2,512,256]{2,1,0:T(8,128)}) fusion(f32[2,512,256]{2,1,0:T(8,128)} %reduce-scatter.2.cloned.1.call-done, pred[512]{0:T(512)(128)(4,1)S(1)} %broadcast_in_dim.53), kind=kLoop, calls=%fused_computation.59 | loop fusion | flops 524288 | bytes 3146240 | tf_op jit(solution)/shard_map/neg | solution.py:76
  120.5 1.0 fusion.19
  122.5 1.0 fusion.10
  123.5 1.0 fusion.11
  125.4 37.0 %all-reduce.2.cloned.1.call-done = f32[2,1,256,256]{3,2,1,0:T(8,128)} async-done(((f32[2,1,256,256]{3,2,1,0:T(8,128)}), f32[2,1,256,256]{3,2,1,0:T(8,128)}) %all-reduce.2.cloned.1.call-update) | async-done | bytes 524304 | tf_op jit(solution)/shard_map/psum | solution.py:84
  162.4 1.9 %sub.26 = f32[2,1,256,256]{3,2,1,0:T(8,128)} subtract(f32[2,1,256,256]{3,2,1,0:T(8,128)S(1)} %copy-done.2, f32[2,1,256,256]{3,2,1,0:T(8,128)} %all-reduce.2.cloned.1.call-done) | non-fusion elementwise | flops 131072 | bytes 1572864 | tf_op jit(solution)/shard_map/sub | solution.py:85
  (56 shorter events, 11.5 us)
Async XLA Ops:
  7.2 34.7 %copy-start = (bf16[2,4,256,256]{3,2,1,0:T(8,128)(2,1)S(1)}, bf16[2,4,256,256]{3,2,1,0:T(8,128)(2,1)}, u32[]{:S(2)}) copy-start(bf16[2,4,256,256]{3,2,1,0:T(8,128)(2,1)} %param.9) | copy-start | bytes 3145732
  7.2 33.1 %all-gather.2.cloned.1.call-start = ((), (), s32[]{:S(2)}) async-start(), calls=%async_computation.2 | async-start | bytes 1310720 | tf_op jit(solution)/shard_map/all_gather | solution.py:34
  7.9 110.0 %reduce-scatter.2.cloned.1.call-start = ((), (), s32[]{:S(2)}) async-start(), calls=%async_computation.3 | async-start | bytes 5242880 | tf_op jit(solution)/shard_map/reduce_scatter | solution.py:68
  40.3 3.0 %copy-start.1 = (bf16[2,4,256,256]{3,2,1,0:T(8,128)(2,1)S(1)}, bf16[2,4,256,256]{3,2,1,0:T(8,128)(2,1)}, u32[]{:S(2)}) copy-start(bf16[2,4,256,256]{3,2,1,0:T(8,128)(2,1)} %all-gather.2.cloned.1.call-done) | copy-start | bytes 3145732
  64.5 41.6 %all-to-all-start = ((bf16[2,4,512,256]{3,2,0,1:T(8,128)(2,1)}), bf16[2,4,512,256]{3,2,0,1:T(8,128)(2,1)S(1)}, u32[]{:S(2)}, u32[]{:S(2)}) async-start(bf16[2,4,512,256]{3,2,0,1:T(8,128)(2,1)} %copy.17), calls=%async_computation.1 | async-start | bytes 4194304 | tf_op jit(solution)/shard_map/all_to_all | solution.py:79
  68.2 94.1 %all-reduce.2.cloned.1.call-start = ((), (), s32[]{:S(2)}) async-start(), calls=%async_computation.4 | async-start | bytes 1048576 | tf_op jit(solution)/shard_map/psum | solution.py:84
  120.4 41.9 %copy-start.2 = (f32[2,1,256,256]{3,2,1,0:T(8,128)S(1)}, f32[2,1,256,256]{3,2,1,0:T(8,128)}, u32[]{:S(2)}) copy-start(f32[2,1,256,256]{3,2,1,0:T(8,128)} %param.10) | copy-start | bytes 1572868
Sparse Core Ops, SparseCore 0:
  9.6 30.6 all-gather.1
  62.4 55.4 reduce-scatter.1
  125.5 36.8 all-reduce.1
where the time goes:
time: 171 us
  waiting for transfers between devices  115 us (67%)
  matrix products  16.1 us (9%)
  between operations  13.9 us (8%)
  other arithmetic  12.6 us (7%)
  local copies, waits for them, and re-layouts  8.88 us (5%)
  starting transfers between devices  3.88 us (2%)
    psum x1, waiting for transfers between devices, local(): total_sum = lax.psum(quad_term, 'prow')  37 us
    all_to_all x1, waiting for transfers between devices, local(): lax.all_to_all(z_rows, 'pcol', split_axis=1, concat_axis=1, tiled=True)  36.9 us
    all_gather x1, waiting for transfers between devices, local(): rows_in = lax.all_gather(panel, 'prow', axis=2, tiled=True)  29.1 us
    reduce_scatter x1, waiting for transfers between devices, local(): lax.psum_scatter(partial_value.reshape(2, rows_all, total_k * block_width...  11.5 us
    dot_general x4, matrix products, one_node(): jnp.einsum('sg,cigw->cisw', table_k, ainv_blocks, preferred_element_type=...  4.94 us
    reshape x1, local copies, waits for them, and re-layouts, local(): partial_value.reshape(2, rows_all, total_k * block_width)  4.76 us
    dynamic_update_slice x4, other arithmetic, local(): per_node = lax.map(one_node, (pick_table, jnp.moveaxis(placed, 1, 0)))  4.27 us
    dot_general x4, matrix products, single(): return jnp.einsum('kra,rkb->kab', left, right, precision=highest)  4.02 us
  transfers between devices with their start and end apart: 4, of which 4 were waited for; matrix products, arithmetic and copies ran while one was open for 4% of the time, Pallas kernels for 0%

commit v1 on v0

--- a/solution.py
+++ b/solution.py
@@ -1,7 +1,26 @@
+import functools
 import jax
 import jax.numpy as jnp
 from jax import lax
 from jax.sharding import PartitionSpec as P
+from jax.lax import axis_size, ppermute
+
+
+def _fit_chunk(mine_x, mesh_name):
+    wide_n = axis_size(mesh_name)
+    response, part_now = (mine_x, 0)
+    while 1 << part_now < wide_n:
+        upper = ppermute(
+            response,
+            axis_name=mesh_name,
+            perm=[(dev_i, dev_i ^ 1 << part_now) for dev_i in range(wide_n)],
+        )
+        response = response + upper
+        part_now = part_now + 1
+    return response
+
+
+step_on_edge = functools.partial(_fit_chunk, mesh_name="prow")
 
 
 def complex_quad(z_part, s_part):
@@ -81,7 +100,7 @@
         received.astype(jnp.float32).reshape(2, n_cols, own_k, rows_all, block_width).sum(axis=1)
     )
     quad_term = complex_quad(z_own, selected.reshape(2, rows_all, own_k, block_width))
-    total_sum = lax.psum(quad_term, "prow")
+    total_sum = step_on_edge(quad_term)
     diag_inv = k_inv - total_sum
     return (sel_inv, diag_inv)
 

time: 171 us -> 172 us (level)
  starting transfers between devices: 3.88 us -> 6.97 us
    psum x1 -> x0, waiting for transfers between devices: 37 us -> none  [local(): total_sum = lax.psum(quad_term, 'prow')]
    ppermute x0 -> x2, waiting for transfers between devices: none -> 35.9 us  [_fit_chunk(): ppermute(response, axis_name=mesh_name, perm=[(dev_i, dev_i ^ 1 << part_n...]
    ppermute x0 -> x2, starting transfers between devices: none -> 3.13 us  [_fit_chunk(): ppermute(response, axis_name=mesh_name, perm=[(dev_i, dev_i ^ 1 << part_n...]
  transfers between devices with their start and end apart: 4 -> 5, of which waited for: 4 -> 5; matrix products, arithmetic and copies ran while one was open for 4% -> 4% of each run, Pallas kernels for 0% -> 0%
where the time goes in v1:
time: 172 us; the launch traced here: 171 us
  waiting for transfers between devices  114 us (66%)
  matrix products  16.1 us (9%)
  between operations  14.2 us (8%)
  other arithmetic  10.9 us (6%)
  local copies, waits for them, and re-layouts  8.88 us (5%)
  starting transfers between devices  6.97 us (4%)
    all_to_all x1, waiting for transfers between devices, local(): lax.all_to_all(z_rows, 'pcol', split_axis=1, concat_axis=1, tiled=True)  37 us
    ppermute x2, waiting for transfers between devices, _fit_chunk(): ppermute(response, axis_name=mesh_name, perm=[(dev_i, dev_i ^ 1 << part_n...  35.9 us
    all_gather x1, waiting for transfers between devices, local(): rows_in = lax.all_gather(panel, 'prow', axis=2, tiled=True)  29.1 us
    reduce_scatter x1, waiting for transfers between devices, local(): lax.psum_scatter(partial_value.reshape(2, rows_all, total_k * block_width...  11.5 us
    dot_general x4, matrix products, one_node(): jnp.einsum('sg,cigw->cisw', table_k, ainv_blocks, preferred_element_type=...  4.94 us
    reshape x1, local copies, waits for them, and re-layouts, local(): partial_value.reshape(2, rows_all, total_k * block_width)  4.76 us
    dynamic_update_slice x4, other arithmetic, local(): per_node = lax.map(one_node, (pick_table, jnp.moveaxis(placed, 1, 0)))  4.27 us
    dot_general x4, matrix products, single(): return jnp.einsum('kra,rkb->kab', left, right, precision=highest)  4.02 us
  transfers between devices with their start and end apart: 5, of which 5 were waited for; matrix products, arithmetic and copies ran while one was open for 4% of the time, Pallas kernels for 0%

profile of v1, /device:TPU:0, one launch (start us, length us, event | category | flops | bytes accessed | tf_op | source)
XLA Modules:
  0.0 171.4 jit_solution(17750377855515778440)
XLA Ops:
  8.0 1.3 reshape.276
  11.2 29.1 %all-gather.2.cloned.1.call-done = bf16[2,4,256,256]{3,2,1,0:T(8,128)(2,1)} async-done(((bf16[2,4,64,256]{3,2,1,0:T(8,128)(2,1)}), bf16[2,4,256,256]{3,2,1,0:T(8,128)(2,1)}) %all-gather.2.cloned.1.call-update) | async-done | bytes 1048592 | tf_op jit(solution)/shard_map/all_gather | solution.py:53
  40.3 1.6 fusion.13
  41.9 1.3 fusion.17
  44.1 13.4 %while.10 = (s32[]{:T(128)}, f32[4,2,512,256]{3,2,1,0:T(8,128)}, bf16[4,1,2]{2,1,0:T(2,128)(2,1)S(1)}, bf16[2,512,2,256]{3,2,1,0:T(2,128)(2,1)S(1)}, bf16[4,2,1,256,256]{4,3,0,2,1:T(8,128)(2,1)S(1)}, /*index=5*/s32[]{:T(128)}) while((s32[]{:T(128)}, f32[4,2,512,256]{3,2,1,0:T(8,128)}, bf16[4,1,2]{2,1,0:T(2,128)(2,1)S(1)}, ...), condition=%wide.region_2.3_spmd, body=%wide.region_1.2_spmd.sunk | while | flops 270008320 | bytes 9962073 | solution.py:82
  44.1 1.2 fusion.43
  46.4 1.0 fusion.48
  47.4 1.2 fusion.43
  49.7 1.1 fusion.48
  50.8 1.2 fusion.43
  53.1 1.1 fusion.48
  54.2 1.2 fusion.43
  56.4 1.0 fusion.48
  57.5 4.8 %copy.21 = f32[4,2,64,8,256]{4,3,0,2,1:T(8,128)} copy(f32[4,2,64,8,256]{4,3,2,1,0:T(8,128)} %bitcast.135) | data formatting | bytes 8388608 | tf_op jit(solution)/shard_map/reshape | solution.py:88
  63.0 1.5 copy.17
  64.5 3.8 %all-to-all-start = ((bf16[2,4,512,256]{3,2,0,1:T(8,128)(2,1)}), bf16[2,4,512,256]{3,2,0,1:T(8,128)(2,1)S(1)}, u32[]{:S(2)}, u32[]{:S(2)}) async-start(bf16[2,4,512,256]{3,2,0,1:T(8,128)(2,1)} %copy.17), calls=%async_computation.1 | async-start | bytes 4194304 | tf_op jit(solution)/shard_map/all_to_all | solution.py:98
  69.1 37.0 %all-to-all-done = bf16[2,4,512,256]{3,2,0,1:T(8,128)(2,1)S(1)} async-done(((bf16[2,4,512,256]{3,2,0,1:T(8,128)(2,1)}), bf16[2,4,512,256]{3,2,0,1:T(8,128)(2,1)S(1)}, u32[]{:S(2)}, u32[]{:S(2)}) %all-to-all-start) | async-done | bytes 2097184 | tf_op jit(solution)/shard_map/all_to_all | solution.py:98
  106.4 11.5 %reduce-scatter.2.cloned.1.call-done = f32[2,512,256]{2,1,0:T(8,128)} async-done(((f32[2,512,1024]{2,1,0:T(8,128)}), f32[2,512,256]{2,1,0:T(8,128)}) %reduce-scatter.2.cloned.1.call-update) | async-done | bytes 1048592 | tf_op jit(solution)/shard_map/reduce_scatter | solution.py:87
  117.9 2.3 %fusion.27 = (f32[2,512,256]{2,1,0:T(8,128)S(1)}, f32[2,512,256]{2,1,0:T(8,128)}) fusion(f32[2,512,256]{2,1,0:T(8,128)} %reduce-scatter.2.cloned.1.call-done, pred[512]{0:T(512)(128)(4,1)S(1)} %broadcast_in_dim.53), kind=kLoop, calls=%fused_computation.61 | loop fusion | flops 524288 | bytes 3146240 | tf_op jit(solution)/shard_map/neg | solution.py:95
  123.5 1.0 fusion.11
  124.6 1.4 collective-permute-start
  126.0 12.5 %collective-permute-done = f32[2,1,256,256]{3,2,1,0:T(8,128)S(1)} collective-permute-done((f32[2,1,256,256]{3,2,1,0:T(8,128)S(1)}, f32[2,1,256,256]{3,2,1,0:T(8,128)S(1)}, u32[]{:S(2)}, u32[]{:S(2)}) %collective-permute-start) | collective-permute-done | bytes 524320 | tf_op jit(solution)/shard_map/ppermute | solution.py:13
  138.5 1.7 collective-permute-start.1
  140.2 23.4 %collective-permute-done.1 = f32[2,1,256,256]{3,2,1,0:T(8,128)S(1)} collective-permute-done((f32[2,1,256,256]{3,2,1,0:T(8,128)S(1)}, f32[2,1,256,256]{3,2,1,0:T(8,128)S(1)}, u32[]{:S(2)}, u32[]{:S(2)}) %collective-permute-start.1) | collective-permute-done | bytes 524320 | tf_op jit(solution)/shard_map/ppermute | solution.py:13
  (58 shorter events, 13.6 us)
Async XLA Ops:
  7.2 34.7 %copy-start = (bf16[2,4,256,256]{3,2,1,0:T(8,128)(2,1)S(1)}, bf16[2,4,256,256]{3,2,1,0:T(8,128)(2,1)}, u32[]{:S(2)}) copy-start(bf16[2,4,256,256]{3,2,1,0:T(8,128)(2,1)} %param.9) | copy-start | bytes 3145732
  7.2 33.1 %all-gather.2.cloned.1.call-start = ((), (), s32[]{:S(2)}) async-start(), calls=%async_computation.2 | async-start | bytes 1310720 | tf_op jit(solution)/shard_map/all_gather | solution.py:53
  7.9 110.0 %reduce-scatter.2.cloned.1.call-start = ((), (), s32[]{:S(2)}) async-start(), calls=%async_computation.3 | async-start | bytes 5242880 | tf_op jit(solution)/shard_map/reduce_scatter | solution.py:87
  40.3 3.0 %copy-start.1 = (bf16[2,4,256,256]{3,2,1,0:T(8,128)(2,1)S(1)}, bf16[2,4,256,256]{3,2,1,0:T(8,128)(2,1)}, u32[]{:S(2)}) copy-start(bf16[2,4,256,256]{3,2,1,0:T(8,128)(2,1)} %all-gather.2.cloned.1.call-done) | copy-start | bytes 3145732
  64.5 41.6 %all-to-all-start = ((bf16[2,4,512,256]{3,2,0,1:T(8,128)(2,1)}), bf16[2,4,512,256]{3,2,0,1:T(8,128)(2,1)S(1)}, u32[]{:S(2)}, u32[]{:S(2)}) async-start(bf16[2,4,512,256]{3,2,0,1:T(8,128)(2,1)} %copy.17), calls=%async_computation.1 | async-start | bytes 4194304 | tf_op jit(solution)/shard_map/all_to_all | solution.py:98
  120.4 43.2 %copy-start.2 = (f32[2,1,256,256]{3,2,1,0:T(8,128)S(1)}, f32[2,1,256,256]{3,2,1,0:T(8,128)}, u32[]{:S(2)}) copy-start(f32[2,1,256,256]{3,2,1,0:T(8,128)} %param.10) | copy-start | bytes 1572868
  124.6 13.9 %collective-permute-start = (f32[2,1,256,256]{3,2,1,0:T(8,128)S(1)}, f32[2,1,256,256]{3,2,1,0:T(8,128)S(1)}, u32[]{:S(2)}, u32[]{:S(2)}) collective-permute-start(f32[2,1,256,256]{3,2,1,0:T(8,128)S(1)} %pad_maximum_fusion), channel_id=1, source_target_pairs={{0,4},{4,0},{8,12},{12,8},{1,5},{5,1},{9,13},{13,9},{2,6},{6,2},{1... | collective-permute-start | bytes 1572872 | tf_op jit(solution)/shard_map/ppermute | solution.py:13
  138.5 25.1 %collective-permute-start.1 = (f32[2,1,256,256]{3,2,1,0:T(8,128)S(1)}, f32[2,1,256,256]{3,2,1,0:T(8,128)S(1)}, u32[]{:S(2)}, u32[]{:S(2)}) collective-permute-start(f32[2,1,256,256]{3,2,1,0:T(8,128)S(1)} %fusion.25), channel_id=1, source_target_pairs={{0,8},{4,12},{8,0},{12,4},{1,9},{5,13},{9,1},{13,5},{2,10},{6,14},... | collective-permute-start | bytes 1572872 | tf_op jit(solution)/shard_map/ppermute | solution.py:13
Sparse Core Ops, SparseCore 0:
  9.6 30.6 all-gather.1
  62.4 55.4 reduce-scatter.1
